TPU v7x, 32 devices: a whole 2x2x4 slice. The times are simulated.
32 devices in a mesh: groups: 2 (over x), tile: 16 (over z, y, core).
Axes of the slice: x: 2, y: 2, z: 4, core: 2. Of those that a mesh axis runs over, the one named last changes fastest.
Arguments:
- tracer: float32 [32, 6, 8, 128, 128], P(('groups', 'tile')), parts along dimension 0, may hold values from -6 to 6
- courant_east: bfloat16 [32, 6, 8, 128, 128], P(('groups', 'tile')), parts along dimension 0, may hold values from -1.5 to 1.5
- courant_north: bfloat16 [32, 6, 8, 128, 128], P(('groups', 'tile')), parts along dimension 0, may hold values from -1.5 to 1.5
- diffusivity: bfloat16 [32, 6, 8, 128, 128], P(('groups', 'tile')), parts along dimension 0, may hold values from 0.049804688 to 5
- seam_table: int32 [6, 4, 3], replicated, may hold values from 0 to 5, as said below
Outputs:
- updated: float32 [32, 6, 8, 128, 128], P(('groups', 'tile')), parts along dimension 0
There are 2 independent parts, one for each index of `groups`. A program takes and returns all parts, laid end to end along the dimension named above; an argument that names none is the same for every part. Nothing has to cross between parts.
Inputs may be any that keep to these rules, and one draw needn't show every extreme that they name: seam_table[p, e] = (q, f, r) names the edge f of panel q != p that borders edge e of panel p, and r is 1 where their edge indices run in opposite directions, 0 otherwise; the 24 edges form 12 pairs whose entries name each other with the same r, as on the faces of a cube ; edge 3 of panel 0 borders edge 3 of panel 1.
All inputs are finite; a program needn't handle non-finite values.
Results may differ from a plain program's by a relative error of at most 0.0003.
Values sent between devices are 32-bit elements; how exact they have to be, the bound alone decides.
A program may use at most 128 MiB of HBM per device.

v0:
```python
import math

import jax
import jax.numpy as jnp
from jax import lax
from jax.sharding import PartitionSpec as P

DEPTH = 2


def padded(block, sides, width):
    for axis, dim in sides:
        count = lax.axis_size(axis)
        forward = [(i, i + 1) for i in range(count - 1)]
        forward.append((count - 1, 0))
        backward = [(target, source) for source, target in forward]
        low = lax.ppermute(
            lax.slice_in_dim(block, block.shape[dim] - width, None, axis=dim), axis, forward
        )
        high = lax.ppermute(lax.slice_in_dim(block, 0, width, axis=dim), axis, backward)
        block = jnp.concatenate([low, block, high], axis=dim)
    return block


def from_behind(value, axis, steps):
    count = lax.axis_size(axis)
    pairs = [(source, (source + steps) % count) for source in range(count)]
    return lax.ppermute(value, axis, pairs)


def edge_strips(panels, rows_deep):
    south_rows = jnp.moveaxis(panels[:, :, :, :rows_deep], 3, 1)
    east_rows = jnp.moveaxis(panels[:, :, ::-1, :][:, :, :rows_deep, :], 2, 1)
    north_rows = jnp.moveaxis(panels[:, :, :, ::-1][:, :, :, :rows_deep], 3, 1)
    west_rows = jnp.moveaxis(panels[:, :, :rows_deep, :], 2, 1)
    return jnp.stack([south_rows, east_rows, north_rows, west_rows], axis=1)


def centered(extended, along):
    kept = extended.shape[along] - 4

    def shifted(offset):
        return lax.slice_in_dim(extended, 2 + offset, 2 + offset + kept, axis=along)

    return (8.0 * (shifted(1) - shifted(-1)) - (shifted(2) - shifted(-2))) / 12.0


def advance(panels, ghosts, courant_east, courant_north, diffusivity):
    west_part = jnp.moveaxis(ghosts[:, 3, ::-1], 1, 2)
    east_part = jnp.moveaxis(ghosts[:, 1], 1, 2)
    south_part = jnp.transpose(ghosts[:, 0, ::-1], (0, 2, 3, 1))
    north_part = jnp.transpose(ghosts[:, 2], (0, 2, 3, 1))
    along_first = jnp.concatenate([west_part, panels, east_part], axis=2)
    along_second = jnp.concatenate([south_part, panels, north_part], axis=3)
    forced = panels - (
        courant_east.astype(jnp.float32) * centered(along_first, 2)
        + courant_north.astype(jnp.float32) * centered(along_second, 3)
    )
    coupling = diffusivity.astype(jnp.float32)
    ratios = []
    partial_values = []
    for height in range(panels.shape[1]):
        diagonal = 1.0 + coupling[:, height]
        if height > 0:
            below = coupling[:, height - 1]
            pivot_value = diagonal + below - below * ratios[-1]
            current = (forced[:, height] + below * partial_values[-1]) / pivot_value
        else:
            pivot_value = diagonal
            current = forced[:, height] / pivot_value
        ratios.append(coupling[:, height] / pivot_value)
        partial_values.append(current)
    solved = [partial_values[-1]]
    for height in range(panels.shape[1] - 2, -1, -1):
        solved.insert(0, partial_values[height] + ratios[height] * solved[0])
    return jnp.stack(solved, axis=1)


def panel_tiles(device, across):
    total = across * across
    tile_offset = jnp.arange(6, dtype=jnp.int32) % 2 * (total // 2 + 1)
    return ((device - tile_offset) % total, tile_offset)


def placement(device, across):
    panel_tile, tile_offset = panel_tiles(device, across)
    row_no = panel_tile // across
    col_no = panel_tile % across
    on_edge = jnp.stack(
        [col_no == 0, row_no == across - 1, col_no == across - 1, row_no == 0], axis=1
    ).reshape(24)
    along_edge = jnp.stack([row_no, col_no, row_no, col_no], axis=1).reshape(24)
    return (on_edge, along_edge, panel_tile, tile_offset)


def device_at(edge_no, spot, across):
    return jnp.where(
        edge_no == 0,
        spot * across,
        jnp.where(
            edge_no == 1,
            (across - 1) * across + spot,
            jnp.where(edge_no == 2, spot * across + across - 1, spot),
        ),
    )


def neighbour_step(edge_no, across):
    return jnp.where(
        edge_no == 0, -1, jnp.where(edge_no == 1, across, jnp.where(edge_no == 2, 1, -across))
    )


def sources(seam_table, own_device, across):
    total = across * across
    on_edge, along_edge, panel_tile, tile_offset = placement(own_device, across)
    flat_table = seam_table.reshape(24, 3)
    ghost_edge = jnp.arange(24, dtype=jnp.int32) % 4
    ghost_panel = jnp.arange(24, dtype=jnp.int32) // 4
    turned_spot = jnp.where(flat_table[:, 2] == 1, across - 1 - along_edge, along_edge)
    far_tile = device_at(flat_table[:, 1], turned_spot, across)
    far_device = (far_tile + jnp.take(tile_offset, flat_table[:, 0])) % total
    near_device = (own_device + neighbour_step(ghost_edge, across)) % total
    source_device = jnp.where(on_edge, far_device, near_device)
    source_block = jnp.where(
        on_edge, flat_table[:, 0] * 4 + flat_table[:, 1], ghost_panel * 4 + (ghost_edge + 2) % 4
    )
    reverse_it = jnp.logical_and(on_edge, flat_table[:, 2] == 1)
    return (on_edge, flat_table, source_device, source_block, reverse_it, panel_tile)


def shards(tracer, courant_east, courant_north, diffusivity, seam_table):
    panels = tracer[0]
    tile_count = lax.axis_size("tile")
    across = math.isqrt(tile_count)
    own_device = lax.axis_index("tile")
    strips = edge_strips(panels, DEPTH)
    blocks = strips.reshape((24,) + strips.shape[2:])
    on_edge, flat_table, source_device, source_block, reverse_it, panel_tile = sources(
        seam_table, own_device, across
    )
    row_no = panel_tile // across
    col_no = panel_tile % across
    side_first = jnp.where(col_no == across - 1, 2, 0).astype(jnp.int32)
    side_second = jnp.where(row_no == 0, 3, 1).astype(jnp.int32)
    first_rows = jnp.take_along_axis(strips, side_first[:, None, None, None, None], axis=1)[:, 0]
    second_rows = jnp.take_along_axis(strips, side_second[:, None, None, None, None], axis=1)[:, 0]
    packed = jnp.concatenate([first_rows, second_rows], axis=0)
    collected = lax.all_gather(packed[None], "tile", axis=0, tiled=True)
    slot_in = jnp.where(flat_table[:, 1] % 2 == 0, 0, 6) + flat_table[:, 0]
    picked = jnp.take(
        collected.reshape((tile_count * 12,) + blocks.shape[1:]),
        source_device * 12 + slot_in,
        axis=0,
        mode="clip",
    )
    picked = jnp.where(reverse_it[:, None, None, None], picked[..., ::-1], picked)
    both_rows = jnp.stack([strips[:, 0], strips[:, 2]], axis=0)
    widened = padded(both_rows, (("tile", 0),), 1)
    from_west = from_behind(strips[:, 1], "tile", across)
    from_east = from_behind(strips[:, 3], "tile", -across)
    inside = jnp.stack([widened[0], from_east, widened[3], from_west], axis=1).reshape(blocks.shape)
    ghosts = jnp.where(on_edge[:, None, None, None], picked, inside)
    updated = advance(
        panels, ghosts.reshape(strips.shape), courant_east[0], courant_north[0], diffusivity[0]
    )
    return updated[None]


def solution(mesh):
    placed = (
        P(("groups", "tile"), None, None, None, None),
        P(("groups", "tile"), None, None, None, None),
        P(("groups", "tile"), None, None, None, None),
        P(("groups", "tile"), None, None, None, None),
        P(),
    )
    return jax.shard_map(
        shards,
        mesh=mesh,
        in_specs=placed,
        out_specs=P(("groups", "tile"), None, None, None, None),
        check_vma=False,
    )
```

profile of v0, /device:TPU:0, one launch (start us, length us, event | category | flops | bytes accessed | tf_op | source)
XLA Modules:
  0.0 114.8 jit_solution(10395726204144280213)
XLA Ops:
  6.6 1.1 slice_bitcast_fusion
  7.7 5.5 %fusion.60 = (f32[6,8,128,2]{3,2,1,0:T(8,128)}, f32[6,8,128,2]{3,2,1,0:T(8,128)S(1)}) fusion(f32[6,8,128,128]{3,2,1,0:T(8,128)} %bitcast.97), kind=kLoop, calls=%fused_computation.177 | loop fusion | bytes 196608 | tf_op jit(solution)/shard_map/slice | solution.py:34
  13.2 0.1 slice.139
  13.3 2.4 %copy.55 = f32[6,8,128,2]{2,3,1,0:T(2,128)S(1)} copy(f32[6,8,128,2]{3,2,1,0:T(8,128)} %get-tuple-element.24) | data formatting | bytes 98304
  15.7 0.1 slice.141
  15.8 1.2 %copy.54 = f32[6,8,128,2]{2,3,1,0:T(2,128)S(1)} copy(f32[6,8,128,2]{3,2,1,0:T(8,128)S(1)} %get-tuple-element.25) | data formatting | bytes 98304
  17.0 0.1 pad_maximum_fusion.4
  17.1 0.6 gather_fusion.3
  17.7 0.6 gather_fusion.2
  18.4 0.1 fusion.28
  18.4 0.1 fusion.27
  18.6 0.7 copy.44
  19.3 3.1 %collective-permute-start.3 = (f32[6,2,8,128]{3,1,2,0:T(2,128)S(1)}, f32[6,2,8,128]{3,1,2,0:T(2,128)S(1)}, u32[]{:S(2)}, u32[]{:S(2)}) collective-permute-start(f32[6,2,8,128]{3,1,2,0:T(2,128)S(1)} %bitcast.107), channel_id=1, source_target_pairs={{0,4},{1,5},{2,6},{3,7},{4,8},{5,9},{6,10},{7,11},{8,12},{9,13},{1... | collective-permute-start | bytes 147464 | tf_op jit(solution)/shard_map/ppermute | solution.py:28
  22.4 2.1 %collective-permute-start.1 = (f32[6,2,8,128]{3,1,2,0:T(2,128)S(1)}, f32[6,2,8,128]{3,1,2,0:T(2,128)S(1)}, u32[]{:S(2)}, u32[]{:S(2)}) collective-permute-start(f32[6,2,8,128]{3,1,2,0:T(2,128)S(1)} %get-tuple-element.22), channel_id=1, source_target_pairs={{0,12},{1,13},{2,14},{3,15},{4,0},{5,1},{6,2},{7,3},{8,4},{9,5},{1... | collective-permute-start | bytes 147464 | tf_op jit(solution)/shard_map/ppermute | solution.py:28
  24.5 4.4 %collective-permute-start.2 = (f32[1,6,2,8,128]{4,3,2,1,0:T(8,128)S(1)}, f32[1,6,2,8,128]{4,3,2,1,0:T(8,128)S(1)}, u32[]{:S(2)}, u32[]{:S(2)}) collective-permute-start(f32[1,6,2,8,128]{4,3,2,1,0:T(8,128)S(1)} %copy.47), channel_id=1, source_target_pairs={{1,0},{2,1},{3,2},{4,3},{5,4},{6,5},{7,6},{8,7},{9,8},{10,9},{11,1... | collective-permute-start | bytes 147464 | tf_op jit(solution)/shard_map/ppermute | solution.py:20
  29.1 0.1 broadcast_in_dim.51
  29.4 0.1 copy.41
  29.6 0.7 gather_fusion
  30.4 2.0 %bitcast_convert_fusion = f32[6,8,128,128]{3,2,1,0:T(8,128)} fusion(bf16[1,6,8,128,128]{4,3,2,1,0:T(8,128)(2,1)S(1)} %copy-done.2), kind=kLoop, calls=%fused_computation.34 | loop fusion | flops 786432 | bytes 4718592 | tf_op jit(solution)/shard_map/convert_element_type | solution.py:59
  32.5 0.1 pad_maximum_fusion.5
  32.7 29.1 %all-gather.3.cloned.1.call-done = f32[192,2,8,128]{3,2,1,0:T(8,128)} async-done(((f32[12,2,8,128]{3,2,1,0:T(8,128)}), f32[192,2,8,128]{3,2,1,0:T(8,128)}) %all-gather.3.cloned.1.call-update) | async-done | bytes 1572880 | tf_op jit(solution)/shard_map/all_gather | solution.py:149
  61.8 2.0 %gather_fusion.1 = f32[24,2,8,128]{3,2,1,0:T(8,128)S(1)} fusion(f32[192,2,8,128]{3,2,1,0:T(8,128)} %all-gather.3.cloned.1.call-done, s32[1024]{0:T(1024)S(1)} %pad_clamp_fusion), kind=kCustom, calls=%fused_computation.3 | custom fusion | bytes 393312 | tf_op jit(solution)/shard_map/jit(_take)/gather | solution.py:151
  63.7 0.1 rev.11
  63.8 0.1 bitcast_select_fusion
  64.0 0.1 rev.12
  64.2 2.2 %copy.58 = f32[6,1,2,8,128]{2,4,3,0,1:T(8,128)} copy(f32[6,1,2,8,128]{4,3,2,1,0:T(8,128)S(1)} %get-tuple-element.26) | data formatting | bytes 98304
  66.4 2.3 %copy.59 = f32[6,1,2,8,128]{2,4,3,0,1:T(8,128)} copy(f32[6,1,2,8,128]{4,3,2,1,0:T(8,128)S(1)} %get-tuple-element.29) | data formatting | bytes 98304
  68.7 26.0 %rev.13 = f32[6,1,2,8,128]{2,4,3,0,1:T(8,128)} reverse(f32[6,1,2,8,128]{2,4,3,0,1:T(8,128)} %copy.59), dimensions={2} | reverse | bytes 98304 | tf_op jit(solution)/shard_map/rev | solution.py:51
  94.6 9.8 %fusion.7 = f32[6,8,128,128]{3,2,1,0:T(8,128)S(1)} fusion(f32[6,8,128,128]{3,2,1,0:T(8,128)S(1)} %bitcast.98, f32[6,8,2,128]{3,2,1,0:T(2,128)S(1)} %bitcast.110, f32[6,8,2,128]{3,2,1,0:T(2,128)S(1)} %bitcast.111, f32[6,8,128,2]{3,2,1,0:T(8,128)} %bitcast.100, f32[6,8,128,2]{3,2,1,0:T(8,128)} %bitcast.99, bf16[1,6,8,128,128]{4,3,2,1,0:T(8,128)(2,1)} %param.9, ...), kind=kLoop, calls=%fused_computation.19 | loop fusion | flops 18874368 | bytes 9633792 | tf_op jit(solution)/shard_map/sub | solution.py:55
  104.5 0.7 fusion.22
  105.2 0.7 add_dynamic-update-slice_fusion
  106.3 1.7 %copy-done.3 = f32[6,8,128,128]{3,2,1,0:T(8,128)} copy-done((f32[6,8,128,128]{3,2,1,0:T(8,128)}, f32[6,8,128,128]{3,2,1,0:T(8,128)S(1)}, u32[]{:S(2)}) %copy-start.3) | copy-done | bytes 3145752
  (52 shorter events, 1.2 us)
Async XLA Ops:
  6.5 55.2 %all-gather.3.cloned.1.call-start = ((), (), s32[]{:S(2)}) async-start(), calls=%async_computation | async-start | bytes 1671168 | tf_op jit(solution)/shard_map/all_gather | solution.py:149
  15.7 13.8 %copy-start.4 = (s32[6,4,3]{0,1,2:T(4,128)S(1)}, s32[6,4,3]{0,1,2:T(4,128)}, u32[]{:S(2)}) copy-start(s32[6,4,3]{0,1,2:T(4,128)} %param.11) | copy-start | bytes 868
  17.0 13.4 %copy-start.2 = (bf16[1,6,8,128,128]{4,3,2,1,0:T(8,128)(2,1)S(1)}, bf16[1,6,8,128,128]{4,3,2,1,0:T(8,128)(2,1)}, u32[]{:S(2)}) copy-start(bf16[1,6,8,128,128]{4,3,2,1,0:T(8,128)(2,1)} %param.10) | copy-start | bytes 4718596
  19.3 13.2 %collective-permute-start.3 = (f32[6,2,8,128]{3,1,2,0:T(2,128)S(1)}, f32[6,2,8,128]{3,1,2,0:T(2,128)S(1)}, u32[]{:S(2)}, u32[]{:S(2)}) collective-permute-start(f32[6,2,8,128]{3,1,2,0:T(2,128)S(1)} %bitcast.107), channel_id=1, source_target_pairs={{0,4},{1,5},{2,6},{3,7},{4,8},{5,9},{6,10},{7,11},{8,12},{9,13},{1... | collective-permute-start | bytes 147464 | tf_op jit(solution)/shard_map/ppermute | solution.py:28
  22.4 10.1 %collective-permute-start.1 = (f32[6,2,8,128]{3,1,2,0:T(2,128)S(1)}, f32[6,2,8,128]{3,1,2,0:T(2,128)S(1)}, u32[]{:S(2)}, u32[]{:S(2)}) collective-permute-start(f32[6,2,8,128]{3,1,2,0:T(2,128)S(1)} %get-tuple-element.22), channel_id=1, source_target_pairs={{0,12},{1,13},{2,14},{3,15},{4,0},{5,1},{6,2},{7,3},{8,4},{9,5},{1... | collective-permute-start | bytes 147464 | tf_op jit(solution)/shard_map/ppermute | solution.py:28
  24.5 8.0 %collective-permute-start = (f32[1,6,2,8,128]{4,3,2,1,0:T(8,128)S(1)}, f32[1,6,2,8,128]{4,3,2,1,0:T(8,128)S(1)}, u32[]{:S(2)}, u32[]{:S(2)}) collective-permute-start(f32[1,6,2,8,128]{4,3,2,1,0:T(8,128)S(1)} %copy.45), channel_id=1, source_target_pairs={{0,1},{1,2},{2,3},{3,4},{4,5},{5,6},{6,7},{7,8},{8,9},{9,10},{10,1... | collective-permute-start | bytes 147464 | tf_op jit(solution)/shard_map/ppermute | solution.py:17
  24.5 8.0 %collective-permute-start.2 = (f32[1,6,2,8,128]{4,3,2,1,0:T(8,128)S(1)}, f32[1,6,2,8,128]{4,3,2,1,0:T(8,128)S(1)}, u32[]{:S(2)}, u32[]{:S(2)}) collective-permute-start(f32[1,6,2,8,128]{4,3,2,1,0:T(8,128)S(1)} %copy.47), channel_id=1, source_target_pairs={{1,0},{2,1},{3,2},{4,3},{5,4},{6,5},{7,6},{8,7},{9,8},{10,9},{11,1... | collective-permute-start | bytes 147464 | tf_op jit(solution)/shard_map/ppermute | solution.py:20
  68.7 26.0 %copy-start = (f32[1,6,8,128,128]{4,3,2,1,0:T(8,128)S(1)}, f32[1,6,8,128,128]{4,3,2,1,0:T(8,128)}, u32[]{:S(2)}) copy-start(f32[1,6,8,128,128]{4,3,2,1,0:T(8,128)} %param.7) | copy-start | bytes 9437188
  94.6 9.9 %copy-start.1 = (f32[6,8,128,128]{3,2,1,0:T(8,128)S(1)}, f32[6,8,128,128]{3,2,1,0:T(8,128)}, u32[]{:S(2)}) copy-start(f32[6,8,128,128]{3,2,1,0:T(8,128)} %bitcast_convert_fusion) | copy-start | bytes 9437188
  106.2 1.7 %copy-start.3 = (f32[6,8,128,128]{3,2,1,0:T(8,128)}, f32[6,8,128,128]{3,2,1,0:T(8,128)S(1)}, u32[]{:S(2)}) copy-start(f32[6,8,128,128]{3,2,1,0:T(8,128)S(1)} %constant_dynamic-update-slice_fusion) | copy-start | bytes 9437188
Sparse Core Ops, SparseCore 0:
  19.4 42.3 all-gather.2
where the time goes:
time: 117 us; the launch traced here: 115 us
  local copies, waits for them, and re-layouts  48 us (41%)
  waiting for transfers between devices  29.1 us (25%)
  other arithmetic  14.3 us (12%)
  between operations  13.7 us (12%)
  starting transfers between devices  9.64 us (8%)
    all_gather x1, waiting for transfers between devices, shards(): collected = lax.all_gather(packed[None], 'tile', axis=0, tiled=True)  29.1 us
    rev x1, local copies, waits for them, and re-layouts, advance(): south_part = jnp.transpose(ghosts[:, 0, ::-1], (0, 2, 3, 1))  26 us
    unnamed x20, local copies, waits for them, and re-layouts  9.93 us
    sub x1, other arithmetic, advance(): panels - (courant_east.astype(jnp.float32) * centered(along_first, 2) + c...  9.84 us
    slice x2, local copies, waits for them, and re-layouts, edge_strips(): north_rows = jnp.moveaxis(panels[:, :, :, ::-1][:, :, :, :rows_deep], 3, 1)  5.6 us
    ppermute x2, starting transfers between devices, from_behind(): return lax.ppermute(value, axis, pairs)  5.2 us
    ppermute x1, starting transfers between devices, padded(): lax.ppermute(lax.slice_in_dim(block, 0, width, axis=dim), axis, backward)  4.44 us
  transfers between devices with their start and end apart: 5, of which 1 were waited for; matrix products, arithmetic and copies ran while one was open for 3% of the time, Pallas kernels for 0%

commit v1 on v0

v1 whole, which is shorter than its diff:
```python
import functools
import math

import jax
import jax.numpy as jnp
from jax import lax
from jax.experimental import pallas as pl
from jax.experimental.pallas import tpu as pltpu
from jax.sharding import PartitionSpec as P

DEPTH = 2


def tile_of(device, parity, total):
    return lax.rem(device + total - parity * (total // 2 + 1) + total, total)


def edge_state(device, parity, total, across):
    tile = tile_of(device, parity, total)
    row, col = tile // across, lax.rem(tile, across)
    on = (col == 0, row == across - 1, col == across - 1, row == 0)
    return on, (row, col, row, col)


def edge_tile(edge, spot, across):
    return (spot * across, (across - 1) * across + spot, spot * across + across - 1, spot)[edge]


def exchange_kernel(total, across, table, tracer, h_out, s_out, q, s, r, d, h,
                    q_sem, send1, r_sem, send2, h_sem, out_sem):
    panels, levels, ct, _ = q.shape
    half = panels // 2
    pieces = DEPTH * levels
    me = lax.axis_index("tile")
    steps = (total - 1, across, 1, total - across)

    for p in range(panels):
        pltpu.make_async_copy(tracer.at[p], q.at[p], q_sem.at[p]).start()

    barrier = pltpu.get_barrier_semaphore()

    def greet(i, carry):
        pl.semaphore_signal(barrier, inc=1, device_id={"tile": lax.rem(me + i, total)},
                            device_id_type=pl.DeviceIdType.MESH)
        return carry

    lax.fori_loop(1, total, greet, 0)

    def remote(src, dst, send, recv, device):
        return pltpu.make_async_remote_copy(
            src_ref=src, dst_ref=dst, send_sem=send, recv_sem=recv,
            device_id={"tile": device}, device_id_type=pl.DeviceIdType.MESH)

    lane_group = lax.broadcasted_iota(jnp.int32, (ct, 128), 1) // 4
    for parity in range(2):
        gathered = jnp.zeros((ct, 128), jnp.float32)
        for n in range(half):
            p = 2 * n + parity
            pltpu.make_async_copy(tracer.at[p], q.at[p], q_sem.at[p]).wait()
            for k in range(levels):
                for depth in range(DEPTH):
                    x = depth * levels + k
                    s[parity, 3, n, x] = q[p, k, depth:depth + 1, :]
                    s[parity, 1, n, x] = q[p, k, ct - 1 - depth:ct - depth, :]
                group = n * levels + k
                turned = pltpu.roll(q[p, k], (group * 4 + DEPTH) % 128, 1)
                gathered = jnp.where(lane_group == group, turned, gathered)
        upright = gathered.T
        for n in range(half):
            for k in range(levels):
                base = (n * levels + k) * 4
                s[parity, 2, n, levels + k] = upright[base:base + 1]
                s[parity, 2, n, k] = upright[base + 1:base + 2]
                s[parity, 0, n, k] = upright[base + 2:base + 3]
                s[parity, 0, n, levels + k] = upright[base + 3:base + 4]
        if parity == 0:
            pl.semaphore_wait(barrier, total - 1)
        on, along = edge_state(me, parity, total, across)
        for e in range(4):
            @pl.when(on[e])
            def _():
                slot = ((parity * 4 + e) * across + along[e]) * half

                def spread(i, carry):
                    x = lax.rem(me + i, pieces)
                    src, dst = s.at[parity, e, :, x], r.at[pl.ds(slot, half)]

                    @pl.when(x != me)
                    def _():
                        remote(src, dst, send1.at[parity, e], r_sem, x).start()

                    @pl.when(x == me)
                    def _():
                        pltpu.make_async_copy(src, dst, r_sem).start()

                    return carry

                lax.fori_loop(0, pieces, spread, 0)
        for e in range(4):
            @pl.when(jnp.logical_not(on[e]))
            def _():
                far = (e + 2) % 4
                remote(s.at[parity, e], h.at[parity, far], send1.at[parity, e],
                       h_sem.at[parity, far], lax.rem(me + steps[e], total)).start()

    pltpu.make_async_copy(s, s_out, out_sem.at[0]).start()

    @pl.when(me < pieces)
    def _():
        pltpu.make_async_copy(r, r, r_sem).wait()
        for parity in range(2):
            for e in range(4):
                for n in range(half):
                    p = 2 * n + parity
                    other, f, turn = table[p, e, 0], table[p, e, 1], table[p, e, 2]
                    base = (lax.rem(other, 2) * 4 + f) * across * half + other // 2
                    for spot in range(across):
                        place = jnp.where(turn == 1, across - 1 - spot, spot)
                        d[((parity * 4 + e) * across + spot) * half + n] = r[base + place * half]
                for spot in range(across):
                    owner = (edge_tile(e, spot, across) + parity * (total // 2 + 1)) % total
                    src = d.at[pl.ds(((parity * 4 + e) * across + spot) * half, half)]
                    dst = h.at[parity, e, :, me]

                    @pl.when(me != owner)
                    def _():
                        remote(src, dst, send2.at[parity, e], h_sem.at[parity, e], owner).start()

                    @pl.when(me == owner)
                    def _():
                        pltpu.make_async_copy(src, dst, h_sem.at[parity, e]).start()

    def drain(ref, sem):
        pltpu.make_async_copy(ref, ref, sem).wait()

    for parity in range(2):
        on, along = edge_state(me, parity, total, across)
        for e in range(4):
            drain(h.at[parity, e], h_sem.at[parity, e])
            base = (parity * 4 + e) * across * half

            @pl.when(jnp.logical_and(on[e], me < pieces))
            def _():
                drain(s.at[parity, e, :, pl.ds(0, pieces - 1)], send1.at[parity, e])
                drain(d.at[pl.ds(base, (across - 1) * half)], send2.at[parity, e])

            @pl.when(jnp.logical_and(on[e], me >= pieces))
            def _():
                drain(s.at[parity, e], send1.at[parity, e])

            @pl.when(jnp.logical_not(on[e]))
            def _():
                drain(s.at[parity, e], send1.at[parity, e])

            @pl.when(jnp.logical_and(jnp.logical_not(on[e]), me < pieces))
            def _():
                drain(d.at[pl.ds(base, across * half)], send2.at[parity, e])

    pltpu.make_async_copy(h, h_out, out_sem.at[1]).start()
    pltpu.make_async_copy(s, s_out, out_sem.at[0]).wait()
    pltpu.make_async_copy(h, h_out, out_sem.at[1]).wait()


def update_kernel(total, across, table, q, east, north, coupling, ghost, own, out, rows, cols):
    _, levels, ct, _ = q.shape
    p = pl.program_id(0)
    parity = lax.rem(p, 2)
    on, _ = edge_state(lax.axis_index("tile"), parity, total, across)
    lane = lax.broadcasted_iota(jnp.int32, (levels, 128), 1)

    def ghosts(e):
        turned = jnp.logical_and(on[e], table[p, e, 2] == 1)
        index = jnp.where(turned, 127 - lane, lane)
        return [jnp.take_along_axis(ghost[0, e, 0, depth], index, axis=1) for depth in range(DEPTH)]

    south, east_rows, north_cols, west = (ghosts(e) for e in range(4))
    below1 = south[0] - own[0, 2, 0, 0]
    below2 = south[1] - own[0, 2, 0, 1]
    above1 = north_cols[0] - own[0, 0, 0, 0]
    above2 = north_cols[1] - own[0, 0, 0, 1]

    @pl.when(p == 0)
    def _():
        rows[...] = jnp.zeros_like(rows)

    rows[pl.ds(0, levels, stride=4), :] = -above1
    rows[pl.ds(1, levels, stride=4), :] = 8.0 * above1 - above2
    rows[pl.ds(2, levels, stride=4), :] = below2 - 8.0 * below1
    rows[pl.ds(3, levels, stride=4), :] = below1
    cols[...] = rows[...].T

    size = 16
    wide = lax.broadcasted_iota(jnp.int32, (size, 128), 1)
    rim = jnp.logical_or(wide < DEPTH, wide >= 128 - DEPTH)
    for start in range(0, ct, size):
        ratios, partials = [], []
        for k in range(levels):
            mid = q[0, k, start:start + size]
            if start == 0:
                ext = jnp.concatenate(
                    [west[1][k:k + 1], west[0][k:k + 1], q[0, k, 0:size + DEPTH]], axis=0)
                near = [ext[o:o + size] for o in (0, 1, 3, 4)]
            elif start + size == ct:
                ext = jnp.concatenate(
                    [q[0, k, start - DEPTH:ct], east_rows[0][k:k + 1], east_rows[1][k:k + 1]], axis=0)
                near = [ext[o:o + size] for o in (0, 1, 3, 4)]
            else:
                near = [q[0, k, start + o:start + o + size] for o in (-2, -1, 1, 2)]
            along_i = 8.0 * (near[2] - near[1]) - (near[3] - near[0])
            along_j = 8.0 * (pltpu.roll(mid, 127, 1) - pltpu.roll(mid, 1, 1)) - (
                pltpu.roll(mid, 126, 1) - pltpu.roll(mid, 2, 1))
            patch = pltpu.roll(cols[start:start + size], (126 - 4 * k) % 128, 1)
            along_j = along_j + jnp.where(rim, patch, 0.0)
            forced = mid - (
                east[0, k, start:start + size].astype(jnp.float32) * along_i
                + north[0, k, start:start + size].astype(jnp.float32) * along_j) * (1.0 / 12.0)
            here = coupling[0, k, start:start + size].astype(jnp.float32)
            if k == 0:
                inverse = 1.0 / (1.0 + here)
                current = forced * inverse
            else:
                inverse = 1.0 / ((1.0 + here) + below * (1.0 - ratios[-1]))
                current = (forced + below * partials[-1]) * inverse
            ratios.append(here * inverse)
            partials.append(current)
            below = here
        value = partials[-1]
        out[0, levels - 1, start:start + size] = value
        for k in range(levels - 2, -1, -1):
            value = partials[k] + ratios[k] * value
            out[0, k, start:start + size] = value


def solution(mesh):
    total = mesh.shape["tile"]
    across = math.isqrt(total)

    def shards(tracer, courant_east, courant_north, diffusivity, seam_table):
        _, panels, levels, ct, _ = tracer.shape
        half, pieces = panels // 2, DEPTH * levels
        strips = (2, 4, half, pieces, 1, ct)
        units = (2 * 4 * across * half, 1, ct)
        anywhere = pl.BlockSpec(memory_space=pl.ANY)
        ghost, own = pl.pallas_call(
            functools.partial(exchange_kernel, total, across),
            out_shape=[jax.ShapeDtypeStruct(strips, jnp.float32)] * 2,
            in_specs=[pl.BlockSpec(memory_space=pltpu.SMEM), anywhere],
            out_specs=[anywhere, anywhere],
            scratch_shapes=[
                pltpu.VMEM(tracer.shape[1:], jnp.float32),
                pltpu.VMEM(strips, jnp.float32),
                pltpu.VMEM(units, jnp.float32),
                pltpu.VMEM(units, jnp.float32),
                pltpu.VMEM(strips, jnp.float32),
                pltpu.SemaphoreType.DMA((panels,)),
                pltpu.SemaphoreType.DMA((2, 4)),
                pltpu.SemaphoreType.DMA,
                pltpu.SemaphoreType.DMA((2, 4)),
                pltpu.SemaphoreType.DMA((2, 4)),
                pltpu.SemaphoreType.DMA((2,)),
            ],
            compiler_params=pltpu.CompilerParams(collective_id=0, has_side_effects=True),
            name="exchange",
        )(seam_table, tracer[0])
        dense = (2, 4, half, DEPTH, levels, ct)
        strip_spec = pl.BlockSpec((1, 4, 1, DEPTH, levels, ct), lambda p: (p % 2, 0, p // 2, 0, 0, 0))
        field = pl.BlockSpec((1, levels, ct, ct), lambda p: (p, 0, 0, 0))
        updated = pl.pallas_call(
            functools.partial(update_kernel, total, across),
            grid=(panels,),
            out_shape=jax.ShapeDtypeStruct(tracer.shape[1:], jnp.float32),
            in_specs=[pl.BlockSpec(memory_space=pltpu.SMEM), field, field, field, field,
                      strip_spec, strip_spec],
            out_specs=field,
            scratch_shapes=[pltpu.VMEM((ct, ct), jnp.float32), pltpu.VMEM((ct, ct), jnp.float32)],
            name="update",
        )(seam_table, tracer[0], courant_east[0], courant_north[0], diffusivity[0],
          ghost.reshape(dense), own.reshape(dense))
        return updated[None]

    placed = P(("groups", "tile"), None, None, None, None)
    return jax.shard_map(
        shards, mesh=mesh, in_specs=(placed, placed, placed, placed, P()), out_specs=placed,
        check_vma=False)
```

time: 117 us -> 28.5 us (0.24); the launches traced: 115 us -> 28.2 us
  local copies, waits for them, and re-layouts: 48 us -> 1.38 us
  waiting for transfers between devices: 29.1 us -> 0 us
  Pallas kernels: 0 us -> 26.8 us
  other arithmetic: 14.3 us -> 0 us
  between operations: 13.7 us -> 0.01 us
  starting transfers between devices: 9.64 us -> 0 us
    all_gather x1 -> x0, waiting for transfers between devices: 29.1 us -> none  [shards(): collected = lax.all_gather(packed[None], 'tile', axis=0, tiled=True)]
    pallas_call x0 -> x2, Pallas kernels: none -> 26.8 us  [the longest x1 17.8 us: shards(): pl.pallas_call(functools.partial(exchange_kernel, total, across), out_sha...]
    rev x3 -> x0, local copies, waits for them, and re-layouts: 26.2 us -> none  [the longest x1 26 us: advance(): south_part = jnp.transpose(ghosts[:, 0, ::-1], (0, 2, 3, 1))]
    sub x1 -> x0, other arithmetic: 9.84 us -> none  [advance(): panels - (courant_east.astype(jnp.float32) * centered(along_first, 2) + c...]
    ppermute x4 -> x0, starting transfers between devices: 9.63 us -> none  [the longest x2 5.2 us: from_behind(): return lax.ppermute(value, axis, pairs)]
    unnamed x20 -> x1, local copies, waits for them, and re-layouts: 9.93 us -> 1.38 us
    slice x4 -> x0, local copies, waits for them, and re-layouts: 5.73 us -> none  [the longest x2 5.6 us: edge_strips(): north_rows = jnp.moveaxis(panels[:, :, :, ::-1][:, :, :, :rows_deep], 3, 1)]
    gather x4 -> x0, local copies, waits for them, and re-layouts: 3.93 us -> none  [the longest x1 1.97 us: shards(): jnp.take(collected.reshape((tile_count * 12,) + blocks.shape[1:]), source...]
  transfers between devices with their start and end apart: 5 -> 0, of which waited for: 1 -> 0; matrix products, arithmetic and copies ran while one was open for 3% -> 0% of each run, Pallas kernels for 0% -> 0%
where the time goes in v1:
time: 28.5 us; the launch traced here: 28.2 us
  Pallas kernels  26.8 us (94%)
  local copies, waits for them, and re-layouts  1.38 us (5%)
    pallas_call x1, Pallas kernels, shards(): pl.pallas_call(functools.partial(exchange_kernel, total, across), out_sha...  17.8 us
    pallas_call x1, Pallas kernels, shards(): pl.pallas_call(functools.partial(update_kernel, total, across), grid=(pan...  8.98 us
    unnamed x1, local copies, waits for them, and re-layouts  1.38 us

profile of v1, /device:TPU:0, one launch (start us, length us, event | category | flops | bytes accessed | tf_op | source)
XLA Modules:
  0.0 28.2 jit_solution(5494861774913421677)
XLA Ops:
  0.0 1.4 %copy.7.table = s32[6,4,3]{2,1,0:T(4,128)} copy(s32[6,4,3]{0,1,2:T(4,128)} %param.9) | data formatting | bytes 576 | tf_op args[4]
  1.4 17.8 %exchange.1 = (f32[2,4,3,16,1,128]{5,4,3,2,1,0:T(1,128)}, f32[2,4,3,16,1,128]{5,4,3,2,1,0:T(1,128)}) custom-call(s32[6,4,3]{2,1,0:T(4,128)} %copy.7.table, f32[6,8,128,128]{3,2,1,0:T(8,128)} %bitcast.7), custom_call_target="tpu_custom_call" | custom-call | tf_op jit(solution)/shard_map/exchange/pallas_call | solution.py:244
  19.2 9.0 %update.1 = f32[6,8,128,128]{3,2,1,0:T(8,128)} custom-call(s32[6,4,3]{2,1,0:T(4,128)} %copy.7.table, f32[6,8,128,128]{3,2,1,0:T(8,128)} %bitcast.8, bf16[6,8,128,128]{3,2,1,0:T(8,128)(2,1)} %bitcast.9, bf16[6,8,128,128]{3,2,1,0:T(8,128)(2,1)} %bitcast.10, bf16[6,8,128,128]{3,2,1,0:T(8,128)(2,1)} %bitcast.11, f32[2,4,3,2,8,128]{5,4,3,2,1,0:T(8,128)} %bitcast.12, ...), custom_call_target="tpu_custom_call" | custom-call | tf_op jit(solution)/shard_map/update/pallas_call | solution.py:268

commit v2 on v1

v2 whole, which is shorter than its diff:
```python
import functools
import math

import jax
import jax.numpy as jnp
from jax import lax
from jax.experimental import pallas as pl
from jax.experimental.pallas import tpu as pltpu
from jax.sharding import PartitionSpec as P

DEPTH = 2


def tile_of(device, parity, total):
    return lax.rem(device + total - parity * (total // 2 + 1) + total, total)


def edge_state(device, parity, total, across):
    tile = tile_of(device, parity, total)
    row, col = tile // across, lax.rem(tile, across)
    on = (col == 0, row == across - 1, col == across - 1, row == 0)
    return on, (row, col, row, col)


def edge_tile(edge, spot, across):
    return (spot * across, (across - 1) * across + spot, spot * across + across - 1, spot)[edge]


def central(q, p, k, start, size):
    ct = q.shape[2]
    mid = q[p, k, start:start + size]
    none = jnp.zeros((DEPTH, 128), jnp.float32)
    if start == 0:
        ext = jnp.concatenate([none, q[p, k, 0:size + DEPTH]], axis=0)
        near = [ext[o:o + size] for o in (0, 1, 3, 4)]
    elif start + size == ct:
        ext = jnp.concatenate([q[p, k, start - DEPTH:ct], none], axis=0)
        near = [ext[o:o + size] for o in (0, 1, 3, 4)]
    else:
        near = [q[p, k, start + o:start + o + size] for o in (-2, -1, 1, 2)]
    along_i = 8.0 * (near[2] - near[1]) - (near[3] - near[0])
    along_j = 8.0 * (pltpu.roll(mid, 127, 1) - pltpu.roll(mid, 1, 1)) - (
        pltpu.roll(mid, 126, 1) - pltpu.roll(mid, 2, 1))
    return mid, along_i, along_j


def solve(forced, coupling, levels):
    ratios, partials = [], []
    for k in range(levels):
        value, here = forced(k), coupling(k)
        if k == 0:
            inverse = 1.0 / (1.0 + here)
            current = value * inverse
        else:
            inverse = 1.0 / ((1.0 + here) + below * (1.0 - ratios[-1]))
            current = (value + below * partials[-1]) * inverse
        ratios.append(here * inverse)
        partials.append(current)
        below = here
    solved = [partials[-1]]
    for k in range(levels - 2, -1, -1):
        solved.insert(0, partials[k] + ratios[k] * solved[0])
    return solved


def update_panel(q, east, north, coupling, u, p):
    _, levels, ct, _ = q.shape
    size = 16
    for start in range(0, ct, size):
        part = pl.ds(start, size)

        def forced(k):
            mid, along_i, along_j = central(q, p, k, start, size)
            return mid - (east[p, k, part].astype(jnp.float32) * along_i
                          + north[p, k, part].astype(jnp.float32) * along_j) * (1.0 / 12.0)

        solved = solve(forced, lambda k: coupling[p, k, part].astype(jnp.float32), levels)
        for k in range(levels):
            u[p, k, part] = solved[k]


def rim_columns(field, parity, half, levels, ct):
    lane_group = lax.broadcasted_iota(jnp.int32, (ct, 128), 1) // 4
    gathered = jnp.zeros((ct, 128), jnp.float32)
    for n in range(half):
        for k in range(levels):
            group = n * levels + k
            turned = pltpu.roll(field[2 * n + parity, k].astype(jnp.float32), (group * 4 + DEPTH) % 128, 1)
            gathered = jnp.where(lane_group == group, turned, gathered)
    return gathered.T


def rim_rows(field, parity, half, levels, ct, out, kind):
    for n in range(half):
        for k in range(levels):
            base = (n * levels + k) * 4
            out[kind, parity, base:base + 2] = field[2 * n + parity, k, ct - 16:ct].astype(jnp.float32)[14:16]
            out[kind, parity, base + 2:base + 4] = field[2 * n + parity, k, 0:16].astype(jnp.float32)[0:2]


def exchange_kernel(total, across, table, tracer, east_in, north_in, coupling_in, h_out, rim_out, u_out,
                    q, east, north, coupling, u, rim, s, r, d, h,
                    q_sem, c_sem, send1, r_sem, send2, h_sem, out_sem, u_sem):
    panels, levels, ct, _ = q.shape
    half = panels // 2
    pieces = DEPTH * levels
    me = lax.axis_index("tile")
    steps = (total - 1, across, 1, total - across)

    for p in range(panels):
        pltpu.make_async_copy(tracer.at[p], q.at[p], q_sem.at[p]).start()
    fields = ((east_in, east), (north_in, north), (coupling_in, coupling))
    for i, (src, dst) in enumerate(fields):
        pltpu.make_async_copy(src, dst, c_sem.at[i]).start()

    barrier = pltpu.get_barrier_semaphore()

    def greet(i, carry):
        pl.semaphore_signal(barrier, inc=1, device_id={"tile": lax.rem(me + i, total)},
                            device_id_type=pl.DeviceIdType.MESH)
        return carry

    lax.fori_loop(1, total, greet, 0)

    def remote(src, dst, send, recv, device):
        return pltpu.make_async_remote_copy(
            src_ref=src, dst_ref=dst, send_sem=send, recv_sem=recv,
            device_id={"tile": device}, device_id_type=pl.DeviceIdType.MESH)

    for parity in range(2):
        for n in range(half):
            p = 2 * n + parity
            pltpu.make_async_copy(tracer.at[p], q.at[p], q_sem.at[p]).wait()
            for k in range(levels):
                for depth in range(DEPTH):
                    x = depth * levels + k
                    s[parity, 3, n, x] = q[p, k, depth:depth + 1, :]
                    s[parity, 1, n, x] = q[p, k, ct - 1 - depth:ct - depth, :]
        upright = rim_columns(q, parity, half, levels, ct)
        rim[0, parity] = upright
        for n in range(half):
            for k in range(levels):
                base = (n * levels + k) * 4
                s[parity, 2, n, levels + k] = upright[base:base + 1]
                s[parity, 2, n, k] = upright[base + 1:base + 2]
                s[parity, 0, n, k] = upright[base + 2:base + 3]
                s[parity, 0, n, levels + k] = upright[base + 3:base + 4]
        if parity == 0:
            pl.semaphore_wait(barrier, total - 1)
        on, along = edge_state(me, parity, total, across)
        for e in range(4):
            @pl.when(on[e])
            def _():
                slot = ((parity * 4 + e) * across + along[e]) * half

                def spread(i, carry):
                    x = lax.rem(me + i, pieces)
                    src, dst = s.at[parity, e, :, x], r.at[pl.ds(slot, half)]

                    @pl.when(x != me)
                    def _():
                        remote(src, dst, send1.at[parity, e], r_sem, x).start()

                    @pl.when(x == me)
                    def _():
                        pltpu.make_async_copy(src, dst, r_sem).start()

                    return carry

                lax.fori_loop(0, pieces, spread, 0)
        for e in range(4):
            @pl.when(jnp.logical_not(on[e]))
            def _():
                far = (e + 2) % 4
                remote(s.at[parity, e], h.at[parity, far], send1.at[parity, e],
                       h_sem.at[parity, far], lax.rem(me + steps[e], total)).start()

    def compute(first, last, parity):
        def one(p, carry):
            update_panel(q, east, north, coupling, u, p)
            pltpu.make_async_copy(u.at[p], u_out.at[p], u_sem.at[p]).start()
            return carry

        lax.fori_loop(first, last, one, 0)
        rim[1, parity] = rim_columns(north, parity, half, levels, ct)
        rim[2, parity] = rim_columns(coupling, parity, half, levels, ct)
        rim_rows(east, parity, half, levels, ct, rim, 3)
        rim_rows(coupling, parity, half, levels, ct, rim, 4)

    for i, (src, dst) in enumerate(fields):
        pltpu.make_async_copy(src, dst, c_sem.at[i]).wait()
    compute(0, half, 0)

    @pl.when(me < pieces)
    def _():
        pltpu.make_async_copy(r, r, r_sem).wait()
        for parity in range(2):
            for e in range(4):
                for n in range(half):
                    p = 2 * n + parity
                    other, f, turn = table[0, e, p], table[1, e, p], table[2, e, p]
                    base = (lax.rem(other, 2) * 4 + f) * across * half + other // 2
                    for spot in range(across):
                        place = jnp.where(turn == 1, across - 1 - spot, spot)
                        d[((parity * 4 + e) * across + spot) * half + n] = r[base + place * half]
                for spot in range(across):
                    owner = (edge_tile(e, spot, across) + parity * (total // 2 + 1)) % total
                    src = d.at[pl.ds(((parity * 4 + e) * across + spot) * half, half)]
                    dst = h.at[parity, e, :, me]

                    @pl.when(me != owner)
                    def _():
                        remote(src, dst, send2.at[parity, e], h_sem.at[parity, e], owner).start()

                    @pl.when(me == owner)
                    def _():
                        pltpu.make_async_copy(src, dst, h_sem.at[parity, e]).start()

    compute(half, panels, 1)
    pltpu.make_async_copy(rim, rim_out, out_sem.at[0]).start()

    def drain(ref, sem):
        pltpu.make_async_copy(ref, ref, sem).wait()

    for parity in range(2):
        on, along = edge_state(me, parity, total, across)
        for e in range(4):
            drain(h.at[parity, e], h_sem.at[parity, e])
            base = (parity * 4 + e) * across * half

            @pl.when(jnp.logical_and(on[e], me < pieces))
            def _():
                drain(s.at[parity, e, :, pl.ds(0, pieces - 1)], send1.at[parity, e])
                drain(d.at[pl.ds(base, (across - 1) * half)], send2.at[parity, e])

            @pl.when(jnp.logical_and(on[e], me >= pieces))
            def _():
                drain(s.at[parity, e], send1.at[parity, e])

            @pl.when(jnp.logical_not(on[e]))
            def _():
                drain(s.at[parity, e], send1.at[parity, e])

            @pl.when(jnp.logical_and(jnp.logical_not(on[e]), me < pieces))
            def _():
                drain(d.at[pl.ds(base, across * half)], send2.at[parity, e])

    pltpu.make_async_copy(h, h_out, out_sem.at[1]).start()
    pltpu.make_async_copy(rim, rim_out, out_sem.at[0]).wait()
    pltpu.make_async_copy(h, h_out, out_sem.at[1]).wait()
    for p in range(panels):
        pltpu.make_async_copy(u.at[p], u_out.at[p], u_sem.at[p]).wait()


def correct_kernel(total, across, table, u, ghost, rim, out, change, cols):
    _, levels, ct, _ = u.shape
    half = ghost.shape[2]
    now = pl.program_id(0)

    @pl.when(now == 0)
    def _():
        lane = lax.broadcasted_iota(jnp.int32, (levels, 128), 1)
        for parity in range(2):
            on, _ = edge_state(lax.axis_index("tile"), parity, total, across)
            change[0, parity] = jnp.zeros((ct, 128), jnp.float32)
            for n in range(half):
                p = 2 * n + parity
                base = n * levels * 4

                def ghosts(e):
                    turned = jnp.logical_and(on[e], table[2, e, p] == 1)
                    index = jnp.where(turned, 127 - lane, lane)
                    return [jnp.take_along_axis(ghost[parity, e, n, depth], index, axis=1)
                            for depth in range(DEPTH)]

                south, east, north, west = (ghosts(e) for e in range(4))
                own = [rim[0, parity, pl.ds(base + c, levels, stride=4)] for c in range(4)]
                sides = ((north[0] - own[2], north[1] - own[3], south[0] - own[1], south[1] - own[0]),
                         (east[0], east[1], west[0], west[1]))
                for way, (above1, above2, below1, below2) in enumerate(sides):
                    values = (-above1, 8.0 * above1 - above2, below2 - 8.0 * below1, below1)
                    for c, value in enumerate(values):
                        change[way, parity, pl.ds(base + c, levels, stride=4)] = value
                for way in range(2):
                    def rows(k):
                        return pl.ds(base + 4 * k, 4)

                    solved = solve(
                        lambda k: change[way, parity, rows(k)] * rim[1 + 2 * way, parity, rows(k)] * (-1.0 / 12.0),
                        lambda k: rim[2 + 2 * way, parity, rows(k)], levels)
                    for k in range(levels):
                        change[way, parity, rows(k)] = solved[k]
            cols[parity] = change[0, parity].T

    size = 16
    wide = lax.broadcasted_iota(jnp.int32, (size, 128), 1)
    edge = jnp.logical_or(wide < DEPTH, wide >= 128 - DEPTH)
    for p in range(2 * half):
        @pl.when(now == p)
        def _():
            parity, n = p % 2, p // 2
            for k in range(levels):
                base = (n * levels + k) * 4
                for start in range(0, ct, size):
                    patch = pltpu.roll(cols[parity, start:start + size], (126 - base) % 128, 1)
                    out[0, k, start:start + size] = u[0, k, start:start + size] + jnp.where(edge, patch, 0.0)
                out[0, k, ct - DEPTH:ct] = out[0, k, ct - DEPTH:ct] + change[1, parity, base:base + 2]
                out[0, k, 0:DEPTH] = out[0, k, 0:DEPTH] + change[1, parity, base + 2:base + 4]


def solution(mesh):
    total = mesh.shape["tile"]
    across = math.isqrt(total)

    def shards(tracer, courant_east, courant_north, diffusivity, seam_table):
        _, panels, levels, ct, _ = tracer.shape
        half, pieces = panels // 2, DEPTH * levels
        strips = (2, 4, half, pieces, 1, ct)
        units = (2 * 4 * across * half, 1, ct)
        rims = (5, 2, ct, ct)
        shape = tracer.shape[1:]
        anywhere = pl.BlockSpec(memory_space=pl.ANY)
        scalars = pl.BlockSpec(memory_space=pltpu.SMEM)
        table = jnp.transpose(seam_table, (2, 1, 0))
        ghost, rim, plain = pl.pallas_call(
            functools.partial(exchange_kernel, total, across),
            out_shape=[jax.ShapeDtypeStruct(dims, jnp.float32) for dims in (strips, rims, shape)],
            in_specs=[scalars] + [anywhere] * 4,
            out_specs=[anywhere] * 3,
            scratch_shapes=[
                pltpu.VMEM(shape, jnp.float32),
                pltpu.VMEM(shape, jnp.bfloat16),
                pltpu.VMEM(shape, jnp.bfloat16),
                pltpu.VMEM(shape, jnp.bfloat16),
                pltpu.VMEM(shape, jnp.float32),
                pltpu.VMEM(rims, jnp.float32),
                pltpu.VMEM(strips, jnp.float32),
                pltpu.VMEM(units, jnp.float32),
                pltpu.VMEM(units, jnp.float32),
                pltpu.VMEM(strips, jnp.float32),
                pltpu.SemaphoreType.DMA((panels,)),
                pltpu.SemaphoreType.DMA((3,)),
                pltpu.SemaphoreType.DMA((2, 4)),
                pltpu.SemaphoreType.DMA,
                pltpu.SemaphoreType.DMA((2, 4)),
                pltpu.SemaphoreType.DMA((2, 4)),
                pltpu.SemaphoreType.DMA((2,)),
                pltpu.SemaphoreType.DMA((panels,)),
            ],
            compiler_params=pltpu.CompilerParams(collective_id=0, has_side_effects=True),
            name="exchange",
        )(table, tracer[0], courant_east[0], courant_north[0], diffusivity[0])
        dense = (2, 4, half, DEPTH, levels, ct)
        field = pl.BlockSpec((1, levels, ct, ct), lambda p: (p, 0, 0, 0))
        whole = pl.BlockSpec(memory_space=pltpu.VMEM)
        updated = pl.pallas_call(
            functools.partial(correct_kernel, total, across),
            grid=(panels,),
            out_shape=jax.ShapeDtypeStruct(shape, jnp.float32),
            in_specs=[scalars, field, whole, whole],
            out_specs=field,
            scratch_shapes=[pltpu.VMEM((2, 2, ct, ct), jnp.float32), pltpu.VMEM((2, ct, ct), jnp.float32)],
            name="correct",
        )(table, plain, ghost.reshape(dense), rim)
        return updated[None]

    placed = P(("groups", "tile"), None, None, None, None)
    return jax.shard_map(
        shards, mesh=mesh, in_specs=(placed, placed, placed, placed, P()), out_specs=placed,
        check_vma=False)
```

time: 28.5 us -> 24.5 us (0.86)
  Pallas kernels: 26.8 us -> 24.2 us
  local copies, waits for them, and re-layouts: 1.38 us -> 0 us
    pallas_call x1, Pallas kernels: 8.98 us -> 6.5 us  [shards(): pl.pallas_call(functools.partial(correct_kernel, total, across), grid=(pa...]
    unnamed x1 -> x0, local copies, waits for them, and re-layouts: 1.38 us -> none
where the time goes in v2:
time: 24.5 us; the launch traced here: 24.3 us
  Pallas kernels  24.2 us (99%)
    pallas_call x1, Pallas kernels, shards(): pl.pallas_call(functools.partial(exchange_kernel, total, across), out_sha...  17.7 us
    pallas_call x1, Pallas kernels, shards(): pl.pallas_call(functools.partial(correct_kernel, total, across), grid=(pa...  6.5 us

profile of v2, /device:TPU:0, one launch (start us, length us, event | category | flops | bytes accessed | tf_op | source)
XLA Modules:
  0.0 24.3 jit_solution(6010634714950653399)
XLA Ops:
  0.0 17.7 %exchange.1 = (f32[2,4,3,16,1,128]{5,4,3,2,1,0:T(1,128)}, f32[5,2,128,128]{3,2,1,0:T(8,128)}, f32[6,8,128,128]{3,2,1,0:T(8,128)}) custom-call(s32[3,4,6]{2,1,0:T(4,128)} %bitcast.12, f32[6,8,128,128]{3,2,1,0:T(8,128)} %bitcast.7, bf16[6,8,128,128]{3,2,1,0:T(8,128)(2,1)} %bitcast.8, bf16[6,8,128,128]{3,2,1,0:T(8,128)(2,1)} %bitcast.9, ...), custom_call_target="tpu_custom_call" | custom-call | tf_op jit(solution)/shard_map/exchange/pallas_call | solution.py:325
  17.8 6.5 %correct.1 = f32[6,8,128,128]{3,2,1,0:T(8,128)} custom-call(s32[3,4,6]{2,1,0:T(4,128)} %bitcast.13, f32[6,8,128,128]{3,2,1,0:T(8,128)} %get-tuple-element.8.u, f32[2,4,3,2,8,128]{5,4,3,2,1,0:T(8,128)} %bitcast.11, f32[5,2,128,128]{3,2,1,0:T(8,128)} %get-tuple-element.10.rim), custom_call_target="tpu_custom_call" | custom-call | tf_op jit(solution)/shard_map/correct/pallas_call | solution.py:356

commit v3 on v2

--- a/solution.py
+++ b/solution.py
@@ -9,6 +9,7 @@
 from jax.sharding import PartitionSpec as P
 
 DEPTH = 2
+VMEM_LIMIT = 59 * 1024 * 1024
 
 
 def tile_of(device, parity, total):
@@ -98,9 +99,9 @@
             out[kind, parity, base + 2:base + 4] = field[2 * n + parity, k, 0:16].astype(jnp.float32)[0:2]
 
 
-def exchange_kernel(total, across, table, tracer, east_in, north_in, coupling_in, h_out, rim_out, u_out,
-                    q, east, north, coupling, u, rim, s, r, d, h,
-                    q_sem, c_sem, send1, r_sem, send2, h_sem, out_sem, u_sem):
+def exchange_kernel(total, across, table, tracer, east_in, north_in, coupling_in, h_out, rim, u,
+                    q, east, north, coupling, s, r, d, h,
+                    q_sem, c_sem, send1, r_sem, send2, h_sem, out_sem):
     panels, levels, ct, _ = q.shape
     half = panels // 2
     pieces = DEPTH * levels
@@ -178,7 +179,6 @@
     def compute(first, last, parity):
         def one(p, carry):
             update_panel(q, east, north, coupling, u, p)
-            pltpu.make_async_copy(u.at[p], u_out.at[p], u_sem.at[p]).start()
             return carry
 
         lax.fori_loop(first, last, one, 0)
@@ -217,7 +217,6 @@
                         pltpu.make_async_copy(src, dst, h_sem.at[parity, e]).start()
 
     compute(half, panels, 1)
-    pltpu.make_async_copy(rim, rim_out, out_sem.at[0]).start()
 
     def drain(ref, sem):
         pltpu.make_async_copy(ref, ref, sem).wait()
@@ -245,67 +244,61 @@
             def _():
                 drain(d.at[pl.ds(base, across * half)], send2.at[parity, e])
 
-    pltpu.make_async_copy(h, h_out, out_sem.at[1]).start()
-    pltpu.make_async_copy(rim, rim_out, out_sem.at[0]).wait()
-    pltpu.make_async_copy(h, h_out, out_sem.at[1]).wait()
-    for p in range(panels):
-        pltpu.make_async_copy(u.at[p], u_out.at[p], u_sem.at[p]).wait()
-
-
-def correct_kernel(total, across, table, u, ghost, rim, out, change, cols):
+    pltpu.make_async_copy(h, h_out, out_sem).start()
+    pltpu.make_async_copy(h, h_out, out_sem).wait()
+
+
+def correct_kernel(total, across, table, u, ghost, rim, result, change, cols, out, out_sem):
     _, levels, ct, _ = u.shape
     half = ghost.shape[2]
-    now = pl.program_id(0)
-
-    @pl.when(now == 0)
-    def _():
-        lane = lax.broadcasted_iota(jnp.int32, (levels, 128), 1)
-        for parity in range(2):
-            on, _ = edge_state(lax.axis_index("tile"), parity, total, across)
-            change[0, parity] = jnp.zeros((ct, 128), jnp.float32)
-            for n in range(half):
-                p = 2 * n + parity
-                base = n * levels * 4
-
-                def ghosts(e):
-                    turned = jnp.logical_and(on[e], table[2, e, p] == 1)
-                    index = jnp.where(turned, 127 - lane, lane)
-                    return [jnp.take_along_axis(ghost[parity, e, n, depth], index, axis=1)
-                            for depth in range(DEPTH)]
-
-                south, east, north, west = (ghosts(e) for e in range(4))
-                own = [rim[0, parity, pl.ds(base + c, levels, stride=4)] for c in range(4)]
-                sides = ((north[0] - own[2], north[1] - own[3], south[0] - own[1], south[1] - own[0]),
-                         (east[0], east[1], west[0], west[1]))
-                for way, (above1, above2, below1, below2) in enumerate(sides):
-                    values = (-above1, 8.0 * above1 - above2, below2 - 8.0 * below1, below1)
-                    for c, value in enumerate(values):
-                        change[way, parity, pl.ds(base + c, levels, stride=4)] = value
-                for way in range(2):
-                    def rows(k):
-                        return pl.ds(base + 4 * k, 4)
-
-                    solved = solve(
-                        lambda k: change[way, parity, rows(k)] * rim[1 + 2 * way, parity, rows(k)] * (-1.0 / 12.0),
-                        lambda k: rim[2 + 2 * way, parity, rows(k)], levels)
-                    for k in range(levels):
-                        change[way, parity, rows(k)] = solved[k]
-            cols[parity] = change[0, parity].T
-
+    lane = lax.broadcasted_iota(jnp.int32, (levels, 128), 1)
     size = 16
     wide = lax.broadcasted_iota(jnp.int32, (size, 128), 1)
     edge = jnp.logical_or(wide < DEPTH, wide >= 128 - DEPTH)
-    for p in range(2 * half):
-        @pl.when(now == p)
-        def _():
-            parity, n = p % 2, p // 2
+    for parity in range(2):
+        on, _ = edge_state(lax.axis_index("tile"), parity, total, across)
+        change[0, parity] = jnp.zeros((ct, 128), jnp.float32)
+        for n in range(half):
+            p = 2 * n + parity
+            base = n * levels * 4
+
+            def ghosts(e):
+                turned = jnp.logical_and(on[e], table[2, e, p] == 1)
+                index = jnp.where(turned, 127 - lane, lane)
+                return [jnp.take_along_axis(ghost[parity, e, n, depth], index, axis=1)
+                        for depth in range(DEPTH)]
+
+            south, east, north, west = (ghosts(e) for e in range(4))
+            own = [rim[0, parity, pl.ds(base + c, levels, stride=4)] for c in range(4)]
+            sides = ((north[0] - own[2], north[1] - own[3], south[0] - own[1], south[1] - own[0]),
+                     (east[0], east[1], west[0], west[1]))
+            for way, (above1, above2, below1, below2) in enumerate(sides):
+                values = (-above1, 8.0 * above1 - above2, below2 - 8.0 * below1, below1)
+                for c, value in enumerate(values):
+                    change[way, parity, pl.ds(base + c, levels, stride=4)] = value
+            for way in range(2):
+                def rows(k):
+                    return pl.ds(base + 4 * k, 4)
+
+                solved = solve(
+                    lambda k: change[way, parity, rows(k)] * rim[1 + 2 * way, parity, rows(k)] * (-1.0 / 12.0),
+                    lambda k: rim[2 + 2 * way, parity, rows(k)], levels)
+                for k in range(levels):
+                    change[way, parity, rows(k)] = solved[k]
+        cols[parity] = change[0, parity].T
+
+        for n in range(half):
+            p = 2 * n + parity
             for k in range(levels):
                 base = (n * levels + k) * 4
                 for start in range(0, ct, size):
                     patch = pltpu.roll(cols[parity, start:start + size], (126 - base) % 128, 1)
-                    out[0, k, start:start + size] = u[0, k, start:start + size] + jnp.where(edge, patch, 0.0)
-                out[0, k, ct - DEPTH:ct] = out[0, k, ct - DEPTH:ct] + change[1, parity, base:base + 2]
-                out[0, k, 0:DEPTH] = out[0, k, 0:DEPTH] + change[1, parity, base + 2:base + 4]
+                    out[p, k, start:start + size] = u[p, k, start:start + size] + jnp.where(edge, patch, 0.0)
+                out[p, k, ct - DEPTH:ct] = out[p, k, ct - DEPTH:ct] + change[1, parity, base:base + 2]
+                out[p, k, 0:DEPTH] = out[p, k, 0:DEPTH] + change[1, parity, base + 2:base + 4]
+            pltpu.make_async_copy(out.at[p], result.at[p], out_sem.at[p]).start()
+    for p in range(2 * half):
+        pltpu.make_async_copy(out.at[p], result.at[p], out_sem.at[p]).wait()
 
 
 def solution(mesh):
@@ -320,20 +313,19 @@
         rims = (5, 2, ct, ct)
         shape = tracer.shape[1:]
         anywhere = pl.BlockSpec(memory_space=pl.ANY)
+        whole = pl.BlockSpec(memory_space=pltpu.VMEM)
         scalars = pl.BlockSpec(memory_space=pltpu.SMEM)
         table = jnp.transpose(seam_table, (2, 1, 0))
         ghost, rim, plain = pl.pallas_call(
             functools.partial(exchange_kernel, total, across),
-            out_shape=[jax.ShapeDtypeStruct(dims, jnp.float32) for dims in (strips, rims, shape)],
-            in_specs=[scalars] + [anywhere] * 4,
-            out_specs=[anywhere] * 3,
+            out_shape=[pltpu.VMEM(dims, jnp.float32) for dims in (strips, rims, shape)],
+            in_specs=[scalars] + [pl.BlockSpec(memory_space=pltpu.HBM)] * 4,
+            out_specs=[whole] * 3,
             scratch_shapes=[
                 pltpu.VMEM(shape, jnp.float32),
                 pltpu.VMEM(shape, jnp.bfloat16),
                 pltpu.VMEM(shape, jnp.bfloat16),
                 pltpu.VMEM(shape, jnp.bfloat16),
-                pltpu.VMEM(shape, jnp.float32),
-                pltpu.VMEM(rims, jnp.float32),
                 pltpu.VMEM(strips, jnp.float32),
                 pltpu.VMEM(units, jnp.float32),
                 pltpu.VMEM(units, jnp.float32),
@@ -344,22 +336,21 @@
                 pltpu.SemaphoreType.DMA,
                 pltpu.SemaphoreType.DMA((2, 4)),
                 pltpu.SemaphoreType.DMA((2, 4)),
-                pltpu.SemaphoreType.DMA((2,)),
-                pltpu.SemaphoreType.DMA((panels,)),
+                pltpu.SemaphoreType.DMA,
             ],
-            compiler_params=pltpu.CompilerParams(collective_id=0, has_side_effects=True),
+            compiler_params=pltpu.CompilerParams(collective_id=0, has_side_effects=True,
+                                                 vmem_limit_bytes=VMEM_LIMIT),
             name="exchange",
         )(table, tracer[0], courant_east[0], courant_north[0], diffusivity[0])
         dense = (2, 4, half, DEPTH, levels, ct)
-        field = pl.BlockSpec((1, levels, ct, ct), lambda p: (p, 0, 0, 0))
-        whole = pl.BlockSpec(memory_space=pltpu.VMEM)
         updated = pl.pallas_call(
             functools.partial(correct_kernel, total, across),
-            grid=(panels,),
             out_shape=jax.ShapeDtypeStruct(shape, jnp.float32),
-            in_specs=[scalars, field, whole, whole],
-            out_specs=field,
-            scratch_shapes=[pltpu.VMEM((2, 2, ct, ct), jnp.float32), pltpu.VMEM((2, ct, ct), jnp.float32)],
+            in_specs=[scalars, whole, whole, whole],
+            out_specs=anywhere,
+            scratch_shapes=[pltpu.VMEM((2, 2, ct, ct), jnp.float32), pltpu.VMEM((2, ct, ct), jnp.float32),
+                            pltpu.VMEM(shape, jnp.float32), pltpu.SemaphoreType.DMA((panels,))],
+            compiler_params=pltpu.CompilerParams(vmem_limit_bytes=VMEM_LIMIT // 2),
             name="correct",
         )(table, plain, ghost.reshape(dense), rim)
         return updated[None]

time: 24.5 us -> 20.7 us (0.84)
  Pallas kernels: 24.2 us -> 20.5 us
    pallas_call x1, Pallas kernels: 6.5 us -> 3.05 us  [shards(): pl.pallas_call(functools.partial(correct_kernel, total, across), out_shap...]
    pallas_call x1, Pallas kernels: 17.7 us -> 17.4 us  [shards(): pl.pallas_call(functools.partial(exchange_kernel, total, across), out_sha...]
where the time goes in v3:
time: 20.7 us; the launch traced here: 20.5 us
  Pallas kernels  20.5 us (99%)
    pallas_call x1, Pallas kernels, shards(): pl.pallas_call(functools.partial(exchange_kernel, total, across), out_sha...  17.4 us
    pallas_call x1, Pallas kernels, shards(): pl.pallas_call(functools.partial(correct_kernel, total, across), out_shap...  3.05 us

profile of v3, /device:TPU:0, one launch (start us, length us, event | category | flops | bytes accessed | tf_op | source)
XLA Modules:
  0.0 20.5 jit_solution(7811848168200348381)
XLA Ops:
  0.0 0.0 copy-start
  0.0 17.4 %exchange.1 = (f32[2,4,3,16,1,128]{5,4,3,2,1,0:T(1,128)S(1)}, f32[5,2,128,128]{3,2,1,0:T(8,128)S(1)}, f32[6,8,128,128]{3,2,1,0:T(8,128)S(1)}) custom-call(s32[3,4,6]{2,1,0:T(4,128)} %bitcast.8, f32[6,8,128,128]{3,2,1,0:T(8,128)} %bitcast.10, bf16[6,8,128,128]{3,2,1,0:T(8,128)(2,1)} %bitcast.11, bf16[6,8,128,128]{3,2,1,0:T(8,128)(2,1)} %bitcast.12, ...), custom_call_target="tpu_custom_call" | custom-call | tf_op jit(solution)/shard_map/exchange/pallas_call | solution.py:319
  17.4 0.0 copy-done
  17.4 3.1 %correct.1 = f32[6,8,128,128]{3,2,1,0:T(8,128)} custom-call(s32[3,4,6]{2,1,0:T(4,128)S(1)} %bitcast.9, f32[6,8,128,128]{3,2,1,0:T(8,128)S(1)} %get-tuple-element.8.u, f32[2,4,3,2,8,128]{5,4,3,2,1,0:T(8,128)S(1)} %bitcast.7, f32[5,2,128,128]{3,2,1,0:T(8,128)S(1)} %get-tuple-element.10.rim), custom_call_target="tpu_custom_call" | custom-call | tf_op jit(solution)/shard_map/correct/pallas_call | solution.py:346
Async XLA Ops:
  0.0 17.4 %copy-start = (s32[6,4,3]{0,1,2:T(4,128)S(1)}, s32[6,4,3]{0,1,2:T(4,128)}, u32[]{:S(2)}) copy-start(s32[6,4,3]{0,1,2:T(4,128)} %param.9) | copy-start | bytes 868
